TPU v7x, 32 devices: a whole 2x2x4 slice. The times are simulated.
32 devices in a mesh: lat: 16 (over z, y, x), batch: 2 (over core).
Axes of the slice: x: 2, y: 2, z: 4, core: 2. Of those that a mesh axis runs over, the one named last changes fastest.
Arguments:
- fields: bfloat16 [2, 192, 384, 384], P('batch', 'lat'), may hold values from -6 to 6
- cotangent: bfloat16 [2, 192, 384, 384], P('batch', 'lat'), may hold values from -6 to 6
- weights: bfloat16 [128, 2, 384, 384], P('lat'), may hold values from -0.21875 to 0.21875
- degree_of: int32 [128], replicated, may hold values from 0 to 127, each once
Outputs:
- grad_fields: bfloat16 [2, 192, 384, 384], P('batch', 'lat')
- grad_weights: bfloat16 [128, 2, 384, 384], P('lat')
Inputs may be any that keep to these rules, and one draw needn't show every extreme that they name: `degree_of`: each degree 0 to 127 is held by exactly one slot.
All inputs are finite; a program needn't handle non-finite values.
Results may differ from a plain program's by a relative error of at most 0.018.
Values may be sent and summed in bfloat16 or wider, within the bound.
A program may use at most 64 MiB of HBM per device.

v0:
```python
import jax
import jax.numpy as jnp
from jax import lax
from jax.sharding import PartitionSpec as P

LATS = 192
LONS = 384
ORDERS = 128
DEGREES = 128
CHANNELS = 384


def legendre_table(order_ids, lat_count, degree_count):
    colatitude = jnp.pi * (jnp.arange(lat_count, dtype=jnp.float32) + 0.5) / lat_count
    cosine = jnp.cos(colatitude)[None, :]
    log_sine = jnp.log(jnp.sin(colatitude))[None, :]
    order_col = order_ids[:, None]
    order_real = order_col.astype(jnp.float32)
    steps_up = jnp.arange(1, degree_count + 1, dtype=jnp.float32)[None, :]
    factor = jnp.where(
        steps_up <= order_real, 0.5 * jnp.log((2.0 * steps_up + 1.0) / (2.0 * steps_up)), 0.0
    )
    log_start = 0.5 * jnp.log(1.0 / (4.0 * jnp.pi)) + jnp.sum(factor, axis=1, keepdims=True)
    diagonal = jnp.exp(log_start + order_real * log_sine)
    squared = order_real * order_real

    def advance(carry, degree):
        previous, older = carry
        degree_real = degree.astype(jnp.float32)
        lead = jnp.sqrt(
            jnp.maximum(4.0 * degree_real * degree_real - 1.0, 0.0)
            / jnp.maximum(degree_real * degree_real - squared, 1.0)
        )
        lower = degree_real - 1.0
        back = jnp.sqrt(
            jnp.maximum(lower * lower - squared, 0.0) / jnp.maximum(4.0 * lower * lower - 1.0, 1.0)
        )
        general = lead * (cosine * previous - back * older)
        first = jnp.sqrt(2.0 * order_real + 3.0) * cosine * previous
        value = jnp.where(
            degree == order_col,
            diagonal,
            jnp.where(
                degree == order_col + 1, first, jnp.where(degree > order_col + 1, general, 0.0)
            ),
        )
        return ((value, previous), value)

    zeros = jnp.zeros((order_ids.shape[0], lat_count), jnp.float32)
    final_state, table = lax.scan(
        advance, (zeros, zeros), jnp.arange(degree_count, dtype=jnp.int32)
    )
    return jnp.transpose(table, (1, 0, 2))


def spectral_tables(start, ord_dev, degree_of):
    order_ids = start + jnp.arange(ord_dev, dtype=jnp.int32)
    mine = legendre_table(order_ids, LATS, DEGREES)
    selector = (degree_of[:, None] == jnp.arange(DEGREES, dtype=jnp.int32)[None, :]).astype(
        jnp.float32
    )
    chosen = jnp.einsum("mli,jl->mji", mine, selector, precision=lax.Precision.HIGHEST)
    colatitude = jnp.pi * (jnp.arange(LATS, dtype=jnp.float32) + 0.5) / LATS
    quadrature = 2.0 * jnp.pi * jnp.pi / LATS * jnp.sin(colatitude)
    return ((chosen * quadrature[None, None, :]).astype(jnp.bfloat16), chosen.astype(jnp.bfloat16))


def fourier_tables(lon_count, order_count):
    lon_ids = jnp.arange(lon_count, dtype=jnp.int32)[:, None]
    order_ids = jnp.arange(order_count, dtype=jnp.int32)[None, :]
    phase = 2.0 * jnp.pi * (lon_ids * order_ids % lon_count).astype(jnp.float32) / lon_count
    forward = (
        jnp.stack([jnp.cos(phase), -jnp.sin(phase)], axis=2).reshape(lon_count, 2 * order_count)
        / lon_count
    )
    doubled = jnp.where(order_ids == 0, 1.0, 2.0)
    inverse = jnp.stack([doubled * jnp.cos(phase), -doubled * jnp.sin(phase)], axis=2).reshape(
        lon_count, 2 * order_count
    )
    return (forward.astype(jnp.bfloat16), jnp.transpose(inverse).astype(jnp.bfloat16))


def to_orders(values):
    return lax.all_to_all(values, "lat", split_axis=1, concat_axis=0, tiled=True)


def to_degrees(values):
    return lax.all_to_all(values, "lat", split_axis=0, concat_axis=1, tiled=True)


def back_to_orders(values):
    return lax.all_to_all(values, "lat", split_axis=1, concat_axis=0, tiled=True)


def to_bands(values):
    return lax.all_to_all(values, "lat", split_axis=0, concat_axis=1, tiled=True)


def product(spec, left, right):
    return jnp.einsum(spec, left, right, preferred_element_type=jnp.float32)


def apply_filter(coeffs, weights):
    c_real = coeffs[:, :, 0]
    c_imag = coeffs[:, :, 1]
    w_real = weights[:, 0]
    w_imag = weights[:, 1]
    f_real = product("jmsc,jcd->jmsd", c_real, w_real) - product("jmsc,jcd->jmsd", c_imag, w_imag)
    f_imag = product("jmsc,jcd->jmsd", c_real, w_imag) + product("jmsc,jcd->jmsd", c_imag, w_real)
    return jnp.stack([f_real, f_imag], axis=2).astype(jnp.bfloat16)


def adjoint_filter(grads, weights):
    g_real = grads[:, :, 0]
    g_imag = grads[:, :, 1]
    w_real = weights[:, 0]
    w_imag = weights[:, 1]
    a_real = product("jmsd,jcd->jmsc", g_real, w_real) + product("jmsd,jcd->jmsc", g_imag, w_imag)
    a_imag = product("jmsd,jcd->jmsc", g_imag, w_real) - product("jmsd,jcd->jmsc", g_real, w_imag)
    return jnp.stack([a_real, a_imag], axis=2).astype(jnp.bfloat16)


def filter_grad(coeffs, grads):
    c_real = coeffs[:, :, 0]
    c_imag = coeffs[:, :, 1]
    g_real = grads[:, :, 0]
    g_imag = grads[:, :, 1]
    dw_real = product("jmsc,jmsd->jcd", c_real, g_real) + product("jmsc,jmsd->jcd", c_imag, g_imag)
    dw_imag = product("jmsc,jmsd->jcd", c_real, g_imag) - product("jmsc,jmsd->jcd", c_imag, g_real)
    return jnp.stack([dw_real, dw_imag], axis=1)


def local(fields, cotangent, weights, degree_of):
    samples = fields.shape[0]
    band_rows = fields.shape[1]
    ord_dev = ORDERS // lax.axis_size("lat")
    forward, inverse = fourier_tables(LONS, ORDERS)
    qslot, pslot = spectral_tables(lax.axis_index("lat") * ord_dev, ord_dev, degree_of)
    spectra = product("sikc,kf->ifsc", fields, forward).astype(jnp.bfloat16)
    spectra = spectra.reshape(band_rows, ORDERS, 2, samples, CHANNELS)
    gathered = to_orders(spectra)
    coeffs_local = product("mji,imrsc->jmrsc", qslot, gathered).astype(jnp.bfloat16)
    coeffs = to_degrees(coeffs_local)
    filtered = apply_filter(coeffs, weights)
    returned = back_to_orders(filtered)
    synth_local = product("mji,jmrsc->imrsc", pslot, returned).astype(jnp.bfloat16)
    synth = to_bands(synth_local)
    response = product(
        "ifsc,fk->sikc", synth.reshape(band_rows, 2 * ORDERS, samples, CHANNELS), inverse
    )
    activated, pullback = jax.vjp(jax.nn.gelu, response)
    upstream = pullback(cotangent.astype(jnp.float32))[0].astype(jnp.bfloat16)
    grad_synth = product("sikc,fk->ifsc", upstream, inverse).astype(jnp.bfloat16)
    grad_synth = grad_synth.reshape(band_rows, ORDERS, 2, samples, CHANNELS)
    grad_gathered = to_orders(grad_synth)
    grad_local = product("mji,imrsc->jmrsc", pslot, grad_gathered).astype(jnp.bfloat16)
    grad_filtered = to_degrees(grad_local)
    weight_total = lax.psum(filter_grad(coeffs, grad_filtered).astype(jnp.bfloat16), "batch")
    grad_coeffs = adjoint_filter(grad_filtered, weights)
    grad_back = back_to_orders(grad_coeffs)
    grad_local_spec = product("mji,jmrsc->imrsc", qslot, grad_back).astype(jnp.bfloat16)
    grad_bands = to_bands(grad_local_spec)
    delta = product(
        "ifsc,kf->sikc", grad_bands.reshape(band_rows, 2 * ORDERS, samples, CHANNELS), forward
    )
    grad_fields = (cotangent.astype(jnp.float32) + delta).astype(jnp.bfloat16)
    return (grad_fields, weight_total)


def solution(mesh):
    return jax.shard_map(
        local,
        mesh=mesh,
        in_specs=(
            P("batch", "lat", None, None),
            P("batch", "lat", None, None),
            P("lat", None, None, None),
            P(),
        ),
        out_specs=(P("batch", "lat", None, None), P("lat", None, None, None)),
        check_vma=False,
    )
```

profile of v0, /device:TPU:12, one launch (start us, length us, event | category | flops | bytes accessed | tf_op | source)
XLA Modules:
  0.0 810.5 jit_solution(15554122631083850034)
XLA Ops:
  12.2 3.7 convert_bitcast_fusion.3
  15.9 4.8 reshape.480
  23.8 7.2 all-to-all-start
  31.3 351.8 %while.21 = (s32[]{:T(128)}, f32[8,192]{1,0:T(8,128)S(1)}, f32[8,192]{1,0:T(8,128)S(1)}, f32[128,8,192]{2,1,0:T(8,128)S(1)}, s32[128]{0:T(128)S(1)}, /*index=5*/...) while((s32[]{:T(128)}, f32[8,192]{1,0:T(8,128)S(1)}, ...), condition=%wide.region_2.3_spmd.clone.clone.clone.clone, body=%wide.region_1.2_spmd.clone.clone.clone.clone.sunk | while | flops 18991 | bytes 48339 | solution.py:50
  390.9 43.5 %all_to_all.126 = bf16[128,8,2,1,384]{4,2,1,3,0:T(2,128)(2,1)S(1)} all-to-all(bf16[128,8,2,1,384]{4,2,1,3,0:T(2,128)(2,1)} %copy.183), channel_id=1, replica_groups=mesh['lat'=16,'batch'=2] {'lat'}, dimensions={0} | all-to-all | bytes 3145728 | tf_op jit(solution)/shard_map/all_to_all | solution.py:88
  439.0 40.7 %all_to_all.127 = bf16[8,128,2,1,384]{4,0,3,2,1:T(8,128)(2,1)S(1)} all-to-all(bf16[8,128,2,1,384]{4,0,3,2,1:T(8,128)(2,1)S(1)} %copy.188), channel_id=1, replica_groups=mesh['lat'=16,'batch'=2] {'lat'}, dimensions={1} | all-to-all | bytes 3145728 | tf_op jit(solution)/shard_map/all_to_all | solution.py:92
  480.4 3.8 copy.190
  484.3 5.8 all-to-all-start.3
  491.4 51.3 %all-to-all-done.3 = bf16[192,8,2,1,384]{4,2,1,3,0:T(2,128)(2,1)} async-done(((bf16[192,8,2,1,384]{4,2,1,3,0:T(2,128)(2,1)}), bf16[192,8,2,1,384]{4,2,1,3,0:T(2,128)(2,1)}, u32[]{:S(2)}, u32[]{:S(2)}) %all-to-all-start.3) | async-done | bytes 2359328 | tf_op jit(solution)/shard_map/all_to_all | solution.py:96
  544.8 3.8 copy.192
  548.6 6.1 reshape.485
  554.7 9.2 %convert_bitcast_fusion.1 = bf16[12,256,1,384]{3,1,0,2:T(8,128)(2,1)} fusion(bf16[384,256,1]{0,1,2:T(8,128)(2,1)S(1)} %reshape.499, bf16[1,12,384,384]{3,2,1,0:T(8,128)(2,1)} %param.7, bf16[12,256,384]{2,1,0:T(8,128)(2,1)} %reshape.485, bf16[384,256]{0,1:T(8,128)(2,1)S(1)} %convert_element_type.174), kind=kOutput, calls=%fused_computation.70 | convolution fusion | flops 1850277888 | bytes 8650752 | tf_op jit(solution)/shard_map/sikc,fk->ifsc/dot_general | solution.py:100
  563.9 5.9 reshape.487
  569.8 3.3 copy.194
  573.1 57.4 %all_to_all.128 = bf16[12,128,2,1,384]{4,2,0,3,1:T(2,128)(2,1)S(1)} all-to-all(bf16[12,128,2,1,384]{4,2,0,3,1:T(2,128)(2,1)S(1)} %copy.194), channel_id=1, replica_groups=mesh['lat'=16,'batch'=2] {'lat'}, dimensions={1} | all-to-all | bytes 4718592 | tf_op jit(solution)/shard_map/all_to_all | solution.py:84
  633.7 4.9 copy.198
  638.6 41.1 %all_to_all.129 = bf16[128,8,2,1,384]{4,2,1,3,0:T(2,128)(2,1)S(1)} all-to-all(bf16[128,8,2,1,384]{4,2,1,3,0:T(2,128)(2,1)} %copy.198), channel_id=1, replica_groups=mesh['lat'=16,'batch'=2] {'lat'}, dimensions={0} | all-to-all | bytes 3145728 | tf_op jit(solution)/shard_map/all_to_all | solution.py:88
  686.2 5.5 all-to-all-start.6
  699.3 28.5 %all-to-all-done.6 = bf16[8,128,2,1,384]{4,0,3,2,1:T(8,128)(2,1)} async-done(((bf16[8,128,2,1,384]{4,0,3,2,1:T(8,128)(2,1)}), bf16[8,128,2,1,384]{4,0,3,2,1:T(8,128)(2,1)}, u32[]{:S(2)}, u32[]{:S(2)}) %all-to-all-start.6) | async-done | bytes 1572896 | tf_op jit(solution)/shard_map/all_to_all | solution.py:92
  730.1 3.8 copy.203
  734.0 4.9 all-to-all-start.7
  739.7 5.1 copy.211
  744.8 47.2 %all-to-all-done.7 = bf16[192,8,2,1,384]{4,2,1,3,0:T(2,128)(2,1)S(1)} async-done(((bf16[192,8,2,1,384]{4,2,1,3,0:T(2,128)(2,1)}), bf16[192,8,2,1,384]{4,2,1,3,0:T(2,128)(2,1)S(1)}, u32[]{:S(2)}, u32[]{:S(2)}) %all-to-all-start.7) | async-done | bytes 2359328 | tf_op jit(solution)/shard_map/all_to_all | solution.py:96
  797.3 5.8 fusion.24
  (981 shorter events, 315.3 us)
Async XLA Ops:
  7.2 5.0 copy-start
  23.8 360.4 %all-to-all-start = ((bf16[12,128,2,1,384]{4,2,0,3,1:T(2,128)(2,1)}), bf16[12,128,2,1,384]{4,2,0,3,1:T(2,128)(2,1)}, u32[]{:S(2)}, u32[]{:S(2)}) async-start(bf16[12,128,2,1,384]{4,2,0,3,1:T(2,128)(2,1)} %copy.178), calls=%async_computation | async-start | bytes 4718592 | tf_op jit(solution)/shard_map/all_to_all | solution.py:84
  30.9 352.6 %copy-start.5 = (s32[128]{0:T(128)S(1)}, s32[128]{0:T(128)}, u32[]{:S(2)}) copy-start(s32[128]{0:T(128)} %param.9) | copy-start | bytes 1540
  386.6 48.4 %slice-start = ((s8[4718592]{0:T(1024)(128)(4,1)}), s8[524288]{0:T(1024)(128)(4,1)S(1)}, s32[]{:S(2)}) async-start(s8[4718592]{0:T(1024)(128)(4,1)} %bitcast.253), calls=%async_computation.9 | async-start | bytes 1048576
  390.9 44.1 %slice-start.1 = ((s8[4718592]{0:T(1024)(128)(4,1)}), s8[4194304]{0:T(1024)(128)(4,1)S(1)}, s32[]{:S(2)}) async-start(s8[4718592]{0:T(1024)(128)(4,1)} %bitcast.253), calls=%async_computation.10 | async-start | bytes 8388608
  484.3 58.4 %all-to-all-start.3 = ((bf16[192,8,2,1,384]{4,2,1,3,0:T(2,128)(2,1)}), bf16[192,8,2,1,384]{4,2,1,3,0:T(2,128)(2,1)}, u32[]{:S(2)}, u32[]{:S(2)}) async-start(bf16[192,8,2,1,384]{4,2,1,3,0:T(2,128)(2,1)} %copy.190), calls=%async_computation.3 | async-start | bytes 4718592 | tf_op jit(solution)/shard_map/all_to_all | solution.py:96
  631.2 49.1 %slice-start.2 = ((s8[4718592]{0:T(1024)(128)(4,1)}), s8[524288]{0:T(1024)(128)(4,1)S(1)}, s32[]{:S(2)}) async-start(s8[4718592]{0:T(1024)(128)(4,1)} %bitcast.255), calls=%async_computation.11 | async-start | bytes 1048576
  638.6 41.7 %slice-start.3 = ((s8[4718592]{0:T(1024)(128)(4,1)}), s8[4194304]{0:T(1024)(128)(4,1)S(1)}, s32[]{:S(2)}) async-start(s8[4718592]{0:T(1024)(128)(4,1)} %bitcast.255), calls=%async_computation.12 | async-start | bytes 8388608
  680.3 2.8 copy-start.2
  686.2 41.6 %all-to-all-start.6 = ((bf16[8,128,2,1,384]{4,0,3,2,1:T(8,128)(2,1)}), bf16[8,128,2,1,384]{4,0,3,2,1:T(8,128)(2,1)}, u32[]{:S(2)}, u32[]{:S(2)}) async-start(bf16[8,128,2,1,384]{4,0,3,2,1:T(8,128)(2,1)} %copy.201), calls=%async_computation.6 | async-start | bytes 3145728 | tf_op jit(solution)/shard_map/all_to_all | solution.py:92
  691.7 48.0 %all-reduce.2.cloned.1.call-start = ((), (), s32[]{:S(2)}) async-start(), calls=%async_computation.8 | async-start | bytes 9437184 | tf_op jit(solution)/shard_map/psum | solution.py:158
  692.0 2.1 copy-start.3
  734.0 4.9 copy-start.4
  734.0 58.0 %all-to-all-start.7 = ((bf16[192,8,2,1,384]{4,2,1,3,0:T(2,128)(2,1)}), bf16[192,8,2,1,384]{4,2,1,3,0:T(2,128)(2,1)S(1)}, u32[]{:S(2)}, u32[]{:S(2)}) async-start(bf16[192,8,2,1,384]{4,2,1,3,0:T(2,128)(2,1)} %copy.203), calls=%async_computation.7 | async-start | bytes 4718592 | tf_op jit(solution)/shard_map/all_to_all | solution.py:96
  797.3 5.8 copy-start.1
Sparse Core Ops, SparseCore 0:
  699.4 30.0 all-reduce.1
where the time goes:
time: 822 us; the launch traced here: 810 us
  other arithmetic  192 us (23%)
  blocking collectives  183 us (22%)
  local copies, waits for them, and re-layouts  147 us (18%)
  waiting for transfers between devices  127 us (15%)
  loops' own time  86.7 us (11%)
  matrix products  37.1 us (5%)
  starting transfers between devices  23.7 us (3%)
  between operations  15 us (2%)
    all_to_all x2, waiting for transfers between devices, to_bands(): lax.all_to_all(values, 'lat', split_axis=0, concat_axis=1, tiled=True)  98.5 us
    another operation x1, loops' own time, legendre_table(): lax.scan(advance, (zeros, zeros), jnp.arange(degree_count, dtype=jnp.int32))  86.7 us
    all_to_all x2, blocking collectives, to_degrees(): lax.all_to_all(values, 'lat', split_axis=0, concat_axis=1, tiled=True)  84.7 us
    gt x128, other arithmetic, advance(): degree > order_col + 1  82.3 us
    eq x128, other arithmetic, advance(): degree == order_col  81.4 us
    dynamic_slice x128, local copies, waits for them, and re-layouts, legendre_table(): lax.scan(advance, (zeros, zeros), jnp.arange(degree_count, dtype=jnp.int32))  79.2 us
    all_to_all x1, blocking collectives, to_orders(): lax.all_to_all(values, 'lat', split_axis=1, concat_axis=0, tiled=True)  57.4 us
    all_to_all x1, blocking collectives, back_to_orders(): lax.all_to_all(values, 'lat', split_axis=1, concat_axis=0, tiled=True)  40.7 us
  transfers between devices with their start and end apart: 5, of which 3 were waited for; matrix products, arithmetic and copies ran while one was open for 35% of the time, Pallas kernels for 0%

commit v1 on v0

--- a/solution.py
+++ b/solution.py
@@ -8,6 +8,12 @@
 ORDERS = 128
 DEGREES = 128
 CHANNELS = 384
+
+
+def trade_parts(x, axis, split, join):
+    parts = jnp.split(x, lax.axis_size(axis), axis=split)
+    received = lax.all_to_all(jnp.stack(parts), axis, 0, 0)
+    return jnp.concatenate(received, axis=join)
 
 
 def legendre_table(order_ids, lat_count, degree_count):
@@ -93,7 +99,7 @@
 
 
 def to_bands(values):
-    return lax.all_to_all(values, "lat", split_axis=0, concat_axis=1, tiled=True)
+    return trade_parts(values, "lat", 0, 1)
 
 
 def product(spec, left, right):

time: 822 us -> 825 us (level)
    reshape x0 -> x2, local copies, waits for them, and re-layouts: none -> 9.33 us  [trade_parts(): return jnp.concatenate(received, axis=join)]
    all_to_all x4 -> x0, local copies, waits for them, and re-layouts: 8.87 us -> none  [to_bands(): lax.all_to_all(values, 'lat', split_axis=0, concat_axis=1, tiled=True)]
    another operation x2 -> x6, local copies, waits for them, and re-layouts: 8.47 us -> 17.1 us
where the time goes in v1:
time: 825 us; the launch traced here: 814 us
  other arithmetic  192 us (23%)
  blocking collectives  183 us (22%)
  local copies, waits for them, and re-layouts  150 us (18%)
  waiting for transfers between devices  127 us (15%)
  loops' own time  86.7 us (11%)
  matrix products  37.1 us (4%)
  starting transfers between devices  23.7 us (3%)
  between operations  15.1 us (2%)
    all_to_all x2, waiting for transfers between devices, trade_parts(): received = lax.all_to_all(jnp.stack(parts), axis, 0, 0)  98.5 us
    another operation x1, loops' own time, legendre_table(): lax.scan(advance, (zeros, zeros), jnp.arange(degree_count, dtype=jnp.int32))  86.7 us
    all_to_all x2, blocking collectives, to_degrees(): lax.all_to_all(values, 'lat', split_axis=0, concat_axis=1, tiled=True)  84.7 us
    gt x128, other arithmetic, advance(): degree > order_col + 1  82.3 us
    eq x128, other arithmetic, advance(): degree == order_col  81.4 us
    dynamic_slice x128, local copies, waits for them, and re-layouts, legendre_table(): lax.scan(advance, (zeros, zeros), jnp.arange(degree_count, dtype=jnp.int32))  79.2 us
    all_to_all x1, blocking collectives, to_orders(): lax.all_to_all(values, 'lat', split_axis=1, concat_axis=0, tiled=True)  57.4 us
    all_to_all x1, blocking collectives, back_to_orders(): lax.all_to_all(values, 'lat', split_axis=1, concat_axis=0, tiled=True)  40.7 us
  transfers between devices with their start and end apart: 5, of which 3 were waited for; matrix products, arithmetic and copies ran while one was open for 35% of the time, Pallas kernels for 0%

profile of v1, /device:TPU:12, one launch (start us, length us, event | category | flops | bytes accessed | tf_op | source)
XLA Modules:
  0.0 813.7 jit_solution(2072125118705137302)
XLA Ops:
  12.2 3.7 convert_bitcast_fusion.3
  15.9 4.8 reshape.482
  23.8 7.2 all-to-all-start
  31.3 351.8 %while.21 = (s32[]{:T(128)}, f32[8,192]{1,0:T(8,128)S(1)}, f32[8,192]{1,0:T(8,128)S(1)}, f32[128,8,192]{2,1,0:T(8,128)S(1)}, s32[128]{0:T(128)S(1)}, /*index=5*/...) while((s32[]{:T(128)}, f32[8,192]{1,0:T(8,128)S(1)}, ...), condition=%wide.region_2.3_spmd.clone.clone.clone.clone, body=%wide.region_1.2_spmd.clone.clone.clone.clone.sunk | while | flops 18991 | bytes 48339 | solution.py:56
  390.9 43.5 %all_to_all.106 = bf16[128,8,2,1,384]{4,2,1,3,0:T(2,128)(2,1)S(1)} all-to-all(bf16[128,8,2,1,384]{4,2,1,3,0:T(2,128)(2,1)} %copy.173), channel_id=1, replica_groups=mesh['lat'=16,'batch'=2] {'lat'}, dimensions={0} | all-to-all | bytes 3145728 | tf_op jit(solution)/shard_map/all_to_all | solution.py:94
  439.0 40.7 %all_to_all.107 = bf16[8,128,2,1,384]{4,0,3,2,1:T(8,128)(2,1)S(1)} all-to-all(bf16[8,128,2,1,384]{4,0,3,2,1:T(8,128)(2,1)S(1)} %copy.178), channel_id=1, replica_groups=mesh['lat'=16,'batch'=2] {'lat'}, dimensions={1} | all-to-all | bytes 3145728 | tf_op jit(solution)/shard_map/all_to_all | solution.py:98
  483.8 5.8 all-to-all-start.3
  490.9 51.3 %all-to-all-done.3 = bf16[16,12,8,2,1,384]{5,2,4,3,1,0:T(8,128)(2,1)} async-done(((bf16[16,12,8,2,1,384]{5,2,4,3,1,0:T(8,128)(2,1)}), bf16[16,12,8,2,1,384]{5,2,4,3,1,0:T(8,128)(2,1)}, u32[]{:S(2)}, u32[]{:S(2)}) %all-to-all-start.3) | async-done | bytes 2359328 | tf_op jit(solution)/shard_map/all_to_all | solution.py:15
  542.2 5.5 copy.181
  547.7 6.1 reshape.488
  553.8 9.2 %convert_bitcast_fusion.1 = bf16[12,256,1,384]{3,1,0,2:T(8,128)(2,1)} fusion(bf16[384,256,1]{0,1,2:T(8,128)(2,1)S(1)} %reshape.503, bf16[1,12,384,384]{3,2,1,0:T(8,128)(2,1)} %param.7, bf16[12,256,384]{2,1,0:T(8,128)(2,1)} %reshape.488, bf16[384,256]{0,1:T(8,128)(2,1)S(1)} %convert_element_type.174), kind=kOutput, calls=%fused_computation.70 | convolution fusion | flops 1850277888 | bytes 8650752 | tf_op jit(solution)/shard_map/sikc,fk->ifsc/dot_general | solution.py:106
  562.9 5.9 reshape.490
  568.9 3.3 copy.183
  572.2 57.4 %all_to_all.108 = bf16[12,128,2,1,384]{4,2,0,3,1:T(2,128)(2,1)S(1)} all-to-all(bf16[12,128,2,1,384]{4,2,0,3,1:T(2,128)(2,1)S(1)} %copy.183), channel_id=1, replica_groups=mesh['lat'=16,'batch'=2] {'lat'}, dimensions={1} | all-to-all | bytes 4718592 | tf_op jit(solution)/shard_map/all_to_all | solution.py:90
  632.7 4.9 copy.187
  637.6 41.1 %all_to_all.109 = bf16[128,8,2,1,384]{4,2,1,3,0:T(2,128)(2,1)S(1)} all-to-all(bf16[128,8,2,1,384]{4,2,1,3,0:T(2,128)(2,1)} %copy.187), channel_id=1, replica_groups=mesh['lat'=16,'batch'=2] {'lat'}, dimensions={0} | all-to-all | bytes 3145728 | tf_op jit(solution)/shard_map/all_to_all | solution.py:94
  685.3 5.5 all-to-all-start.6
  698.4 28.5 %all-to-all-done.6 = bf16[8,128,2,1,384]{4,0,3,2,1:T(8,128)(2,1)} async-done(((bf16[8,128,2,1,384]{4,0,3,2,1:T(8,128)(2,1)}), bf16[8,128,2,1,384]{4,0,3,2,1:T(8,128)(2,1)}, u32[]{:S(2)}, u32[]{:S(2)}) %all-to-all-start.6) | async-done | bytes 1572896 | tf_op jit(solution)/shard_map/all_to_all | solution.py:98
  732.6 4.9 all-to-all-start.7
  738.3 5.1 copy.199
  743.4 47.2 %all-to-all-done.7 = bf16[16,12,8,2,1,384]{5,2,4,3,1,0:T(8,128)(2,1)S(1)} async-done(((bf16[16,12,8,2,1,384]{5,2,4,3,1,0:T(8,128)(2,1)}), bf16[16,12,8,2,1,384]{5,2,4,3,1,0:T(8,128)(2,1)S(1)}, u32[]{:S(2)}, u32[]{:S(2)}) %all-to-all-start.7) | async-done | bytes 2359328 | tf_op jit(solution)/shard_map/all_to_all | solution.py:15
  790.6 3.8 copy.193
  794.5 6.1 reshape.496
  800.6 5.8 fusion.24
  (1011 shorter events, 314.5 us)
Async XLA Ops:
  7.2 5.0 copy-start
  23.8 360.4 %all-to-all-start = ((bf16[12,128,2,1,384]{4,2,0,3,1:T(2,128)(2,1)}), bf16[12,128,2,1,384]{4,2,0,3,1:T(2,128)(2,1)}, u32[]{:S(2)}, u32[]{:S(2)}) async-start(bf16[12,128,2,1,384]{4,2,0,3,1:T(2,128)(2,1)} %copy.168), calls=%async_computation | async-start | bytes 4718592 | tf_op jit(solution)/shard_map/all_to_all | solution.py:90
  30.9 352.6 %copy-start.5 = (s32[128]{0:T(128)S(1)}, s32[128]{0:T(128)}, u32[]{:S(2)}) copy-start(s32[128]{0:T(128)} %param.9) | copy-start | bytes 1540
  386.6 48.4 %slice-start = ((s8[4718592]{0:T(1024)(128)(4,1)}), s8[524288]{0:T(1024)(128)(4,1)S(1)}, s32[]{:S(2)}) async-start(s8[4718592]{0:T(1024)(128)(4,1)} %bitcast.377), calls=%async_computation.9 | async-start | bytes 1048576
  390.9 44.1 %slice-start.1 = ((s8[4718592]{0:T(1024)(128)(4,1)}), s8[4194304]{0:T(1024)(128)(4,1)S(1)}, s32[]{:S(2)}) async-start(s8[4718592]{0:T(1024)(128)(4,1)} %bitcast.377), calls=%async_computation.10 | async-start | bytes 8388608
  483.8 58.4 %all-to-all-start.3 = ((bf16[16,12,8,2,1,384]{5,2,4,3,1,0:T(8,128)(2,1)}), bf16[16,12,8,2,1,384]{5,2,4,3,1,0:T(8,128)(2,1)}, u32[]{:S(2)}, u32[]{:S(2)}) async-start(bf16[16,12,8,2,1,384]{5,2,4,3,1,0:T(8,128)(2,1)} %copy.180), calls=%async_computation.3 | async-start | bytes 4718592 | tf_op jit(solution)/shard_map/all_to_all | solution.py:15
  630.3 49.1 %slice-start.2 = ((s8[4718592]{0:T(1024)(128)(4,1)}), s8[524288]{0:T(1024)(128)(4,1)S(1)}, s32[]{:S(2)}) async-start(s8[4718592]{0:T(1024)(128)(4,1)} %bitcast.379), calls=%async_computation.11 | async-start | bytes 1048576
  637.6 41.7 %slice-start.3 = ((s8[4718592]{0:T(1024)(128)(4,1)}), s8[4194304]{0:T(1024)(128)(4,1)S(1)}, s32[]{:S(2)}) async-start(s8[4718592]{0:T(1024)(128)(4,1)} %bitcast.379), calls=%async_computation.12 | async-start | bytes 8388608
  679.3 2.8 copy-start.2
  685.3 41.6 %all-to-all-start.6 = ((bf16[8,128,2,1,384]{4,0,3,2,1:T(8,128)(2,1)}), bf16[8,128,2,1,384]{4,0,3,2,1:T(8,128)(2,1)}, u32[]{:S(2)}, u32[]{:S(2)}) async-start(bf16[8,128,2,1,384]{4,0,3,2,1:T(8,128)(2,1)} %copy.190), calls=%async_computation.6 | async-start | bytes 3145728 | tf_op jit(solution)/shard_map/all_to_all | solution.py:98
  690.8 47.5 %all-reduce.2.cloned.1.call-start = ((), (), s32[]{:S(2)}) async-start(), calls=%async_computation.8 | async-start | bytes 9437184 | tf_op jit(solution)/shard_map/psum | solution.py:164
  691.1 2.1 copy-start.3
  732.6 4.9 copy-start.4
  732.6 58.0 %all-to-all-start.7 = ((bf16[16,12,8,2,1,384]{5,2,4,3,1,0:T(8,128)(2,1)}), bf16[16,12,8,2,1,384]{5,2,4,3,1,0:T(8,128)(2,1)S(1)}, u32[]{:S(2)}, u32[]{:S(2)}) async-start(bf16[16,12,8,2,1,384]{5,2,4,3,1,0:T(8,128)(2,1)} %copy.192), calls=%async_computation.7 | async-start | bytes 4718592 | tf_op jit(solution)/shard_map/all_to_all | solution.py:15
  800.6 5.8 copy-start.1
Sparse Core Ops, SparseCore 0:
  698.5 30.0 all-reduce.1
